TPU v7x, 32 devices: a whole 2x2x4 slice. The times are simulated.
32 devices in a mesh: node: 8 (over y, x, core), grp: 4 (over z).
Axes of the slice: x: 2, y: 2, z: 4, core: 2. Of those that a mesh axis runs over, the one named last changes fastest.
Arguments:
- tokens: bfloat16 [12288, 1792], P(('node', 'grp')), may hold values from -6 to 6
- cotangent: bfloat16 [12288, 1792], P(('node', 'grp')), may hold values from -6 to 6
- gate_weight: bfloat16 [1792, 1024], P('node'), may hold values from -0.125 to 0.125
- up_weight: bfloat16 [1792, 1024], P('node'), may hold values from -0.125 to 0.125
- down_weight_t: bfloat16 [1792, 1024], P('node'), may hold values from -0.125 to 0.125
- error_memory: bfloat16 [4, 1792, 3072], P('grp', 'node'), may hold values from -4 to 4
- q_init: float32 [3, 1024, 32], replicated, may hold values from -6 to 6
Outputs:
- token_grad: bfloat16 [12288, 1792], P(('node', 'grp'))
- new_error: bfloat16 [4, 1792, 3072], P('grp', 'node')
- p_hat: float32 [3, 1792, 32], P(None, 'node')
- q_new: float32 [3, 1024, 32], replicated
All inputs are finite; a program needn't handle non-finite values.
Results may differ from a plain program's by a relative error of at most 0.012.
Values may be sent and summed in bfloat16 or wider, within the bound.
A program may use at most 192 MiB of HBM per device.

v0:
```python
import math
import jax
import jax.numpy as jnp
from jax import lax
from jax.sharding import PartitionSpec as P


def gelu_parts(value):
    coeff = math.sqrt(2.0 / math.pi)
    inner = coeff * (value + 0.044715 * value * value * value)
    tanh_value = jnp.tanh(inner)
    activation = 0.5 * value * (1.0 + tanh_value)
    slope = 0.5 * (1.0 + tanh_value) + 0.5 * value * (1.0 - tanh_value * tanh_value) * coeff * (
        1.0 + 3.0 * 0.044715 * value * value
    )
    return (activation, slope)


def contract_rows(left_side, right_side):
    return lax.dot_general(
        left_side, right_side, (((0,), (0,)), ((), ())), preferred_element_type=jnp.float32
    )


def on_device(tokens, cotangent, gate_weight, up_weight, down_weight_t, error_memory, q_init):
    node_count = lax.axis_size("node")
    group_count = lax.axis_size("grp")
    hidden_units = gate_weight.shape[1]
    highest = lax.Precision.HIGHEST
    full_gate, full_up, full_down = (
        lax.all_gather(gate_weight, "node", axis=0, tiled=True),
        lax.all_gather(up_weight, "node", axis=0, tiled=True),
        lax.all_gather(down_weight_t, "node", axis=0, tiled=True),
    )
    gate_pre = jnp.dot(tokens, full_gate, preferred_element_type=jnp.float32)
    up_pre = jnp.dot(tokens, full_up, preferred_element_type=jnp.float32)
    activation, slope = gelu_parts(gate_pre)
    hidden = (activation * up_pre).astype(jnp.bfloat16)
    back_hidden = jnp.dot(cotangent, full_down, preferred_element_type=jnp.float32)
    grad_up = (back_hidden * activation).astype(jnp.bfloat16)
    grad_gate = (back_hidden * up_pre * slope).astype(jnp.bfloat16)
    token_grad = (
        lax.dot_general(
            grad_gate, full_gate, (((1,), (1,)), ((), ())), preferred_element_type=jnp.float32
        )
        + lax.dot_general(
            grad_up, full_up, (((1,), (1,)), ((), ())), preferred_element_type=jnp.float32
        )
    ).astype(jnp.bfloat16)
    gate_up = jnp.concatenate([grad_gate, grad_up], axis=1)
    token_cols, cot_cols = (
        lax.all_to_all(tokens, "node", split_axis=1, concat_axis=0, tiled=True),
        lax.all_to_all(cotangent, "node", split_axis=1, concat_axis=0, tiled=True),
    )
    piece_gu = lax.all_gather(gate_up, "node", axis=0, tiled=True)
    piece_hidden = lax.all_gather(hidden, "node", axis=0, tiled=True)
    summed = jnp.concatenate(
        [contract_rows(token_cols, piece_gu), contract_rows(cot_cols, piece_hidden)], axis=1
    )
    grad_scale = 1.0 / math.sqrt(tokens.shape[0] * node_count)
    merged = summed * grad_scale + error_memory[0].astype(jnp.float32)
    blocks = [merged[:, m * hidden_units : (m + 1) * hidden_units] for m in range(3)]
    row_terms = jnp.stack([jnp.dot(blocks[m], q_init[m], precision=highest) for m in range(3)])
    power_rows = lax.psum(row_terms.astype(jnp.bfloat16), "grp").astype(jnp.float32) / group_count
    local_gram = jnp.einsum("mdr,mds->mrs", power_rows, power_rows, precision=highest)
    gram_matrix = lax.psum(local_gram, "node")
    hats = []
    for m in range(3):
        factor = jnp.linalg.cholesky(gram_matrix[m])
        hats.append(jax.scipy.linalg.solve_triangular(factor, power_rows[m].T, lower=True).T)
    col_terms = jnp.stack([jnp.dot(blocks[m].T, hats[m], precision=highest) for m in range(3)])
    q_new = lax.psum(col_terms, ("node", "grp")) / group_count
    errors = [blocks[m] - jnp.dot(hats[m], q_new[m].T, precision=highest) for m in range(3)]
    new_error = jnp.concatenate(errors, axis=1).astype(jnp.bfloat16)[None]
    return (token_grad, new_error, jnp.stack(hats), q_new)


def solution(mesh):
    return jax.shard_map(
        on_device,
        mesh=mesh,
        in_specs=(
            P(("node", "grp"), None),
            P(("node", "grp"), None),
            P("node", None),
            P("node", None),
            P("node", None),
            P("grp", "node", None),
            P(),
        ),
        out_specs=(P(("node", "grp"), None), P("grp", "node", None), P(None, "node", None), P()),
        check_vma=False,
    )
```

profile of v0, /device:TPU:0, one launch (start us, length us, event | category | flops | bytes accessed | tf_op | source)
XLA Modules:
  0.0 512.1 jit_solution(15546751805123783097)
XLA Ops:
  7.2 0.7 all-gather.6.cloned.1.call-update
  7.9 0.7 all-gather.10.cloned.1.call-update
  8.7 0.7 all-gather.8.cloned.1.call-update
  9.4 37.6 %all-gather.6.cloned.1.call-done = bf16[1792,1024]{1,0:T(8,128)(2,1)} async-done(((bf16[224,1024]{1,0:T(8,128)(2,1)}), bf16[1792,1024]{1,0:T(8,128)(2,1)}) %all-gather.6.cloned.1.call-update) | async-done | bytes 3670032 | tf_op jit(solution)/shard_map/all_gather | solution.py:33
  47.0 5.2 %fusion.44 = f32[384,1024]{1,0:T(8,128)} fusion(bf16[384,1792]{1,0:T(8,128)(2,1)} %param.11, bf16[1792,1024]{1,0:T(8,128)(2,1)} %all-gather.6.cloned.1.call-done), kind=kOutput, calls=%fused_computation.92 | convolution fusion | flops 1409286144 | bytes 6619136 | tf_op jit(solution)/shard_map/dot_general | solution.py:39
  52.2 31.1 %all-gather.10.cloned.1.call-done = bf16[1792,1024]{1,0:T(8,128)(2,1)} async-done(((bf16[224,1024]{1,0:T(8,128)(2,1)}), bf16[1792,1024]{1,0:T(8,128)(2,1)}) %all-gather.10.cloned.1.call-update) | async-done | bytes 3670032 | tf_op jit(solution)/shard_map/all_gather | solution.py:31
  83.3 4.8 fusion.45
  88.1 31.5 %all-gather.8.cloned.1.call-done = bf16[1792,1024]{1,0:T(8,128)(2,1)} async-done(((bf16[224,1024]{1,0:T(8,128)(2,1)}), bf16[1792,1024]{1,0:T(8,128)(2,1)}) %all-gather.8.cloned.1.call-update) | async-done | bytes 3670032 | tf_op jit(solution)/shard_map/all_gather | solution.py:32
  119.6 6.4 %multiply_convert_fusion = (bf16[384,1024]{1,0:T(8,128)(2,1)}, bf16[384,1024]{1,0:T(8,128)(2,1)S(1)}, bf16[384,1024]{1,0:T(8,128)(2,1)S(1)}) fusion(f32[384,1024]{1,0:T(8,128)} %fusion.45, f32[384,1024]{1,0:T(8,128)} %fusion.44, bf16[384,1792]{1,0:T(8,128)(2,1)S(1)} %copy-done.2, bf16[1792,1024]{1,0:T(8,128)(2,1)} %all-gather.8.cloned.1.call-done), kind=kOutput, calls=%fused_computation.15 | convolution fusion | flops 1419116544 | bytes 10551296 | tf_op jit(solution)/shard_map/dot_general | solution.py:36
  126.1 0.8 copy-done.7
  126.9 1.4 pad_maximum_fusion
  128.3 1.3 copy-done.1
  129.6 1.5 copy.17
  131.1 3.6 all-to-all-start.1
  134.7 1.5 copy.15
  136.3 24.3 %all-to-all-done.1 = bf16[384,8,224]{0,2,1:T(8,128)(2,1)S(1)} async-done(((bf16[384,8,224]{0,2,1:T(8,128)(2,1)}), bf16[384,8,224]{0,2,1:T(8,128)(2,1)S(1)}, u32[]{:S(2)}, u32[]{:S(2)}) %all-to-all-start.1) | async-done | bytes 1376288 | tf_op jit(solution)/shard_map/all_to_all | solution.py:53
  160.5 3.6 all-to-all-start
  164.3 1.3 copy.25
  165.7 31.9 %all-to-all-done = bf16[384,8,224]{0,2,1:T(8,128)(2,1)S(1)} async-done(((bf16[384,8,224]{0,2,1:T(8,128)(2,1)}), bf16[384,8,224]{0,2,1:T(8,128)(2,1)S(1)}, u32[]{:S(2)}, u32[]{:S(2)}) %all-to-all-start) | async-done | bytes 1376288 | tf_op jit(solution)/shard_map/all_to_all | solution.py:52
  197.6 1.3 copy.24
  198.9 5.4 %fusion.46 = f32[384,1792]{1,0:T(8,128)} fusion(bf16[384,1024]{1,0:T(8,128)(2,1)S(1)} %copy-done.8, bf16[1792,1024]{1,0:T(8,128)(2,1)} %all-gather.10.cloned.1.call-done), kind=kOutput, calls=%fused_computation.94 | convolution fusion | flops 1409286144 | bytes 7208960 | tf_op jit(solution)/shard_map/dot_general | solution.py:43
  204.3 5.4 %convolution_bitcast_fusion.1 = f32[224,1024]{1,0:T(8,128)} fusion(bf16[3072,224]{0,1:T(8,128)(2,1)S(1)} %bitcast.133, bf16[3072,1024]{1,0:T(8,128)(2,1)} %all-gather.14.cloned.1.call-done), kind=kOutput, calls=%fused_computation.19 | convolution fusion | flops 1409286144 | bytes 8585216 | tf_op jit(solution)/shard_map/dot_general | solution.py:20
  209.7 64.7 %all-gather.12.cloned.1.call-done = bf16[3072,2048]{1,0:T(8,128)(2,1)} async-done(((bf16[384,2048]{1,0:T(8,128)(2,1)}), bf16[3072,2048]{1,0:T(8,128)(2,1)}) %all-gather.12.cloned.1.call-update) | async-done | bytes 12582928 | tf_op jit(solution)/shard_map/all_gather | solution.py:55
  274.4 6.4 %convolution_bitcast_fusion = f32[224,2048]{1,0:T(8,128)S(1)} fusion(bf16[3072,224]{0,1:T(8,128)(2,1)S(1)} %bitcast.134, bf16[3072,2048]{1,0:T(8,128)(2,1)} %all-gather.12.cloned.1.call-done), kind=kOutput, calls=%fused_computation.4 | convolution fusion | flops 2818572288 | bytes 15794176 | tf_op jit(solution)/shard_map/dot_general | solution.py:20
  281.8 0.9 fusion.17
  282.7 0.9 fusion.16
  283.6 0.9 fusion.15
  284.5 0.6 pad_maximum_fusion.4
  285.2 20.5 %psum.21 = bf16[3,224,32]{1,2,0:T(8,128)(2,1)} all-reduce(bf16[3,224,32]{1,2,0:T(8,128)(2,1)} %pad_maximum_fusion.4), channel_id=1, replica_groups=mesh['node'=8,'grp'=4] {'grp'}, use_global_device_ids=true, to_apply=%region_0.0 | all-reduce | flops 21504 | bytes 86016 | tf_op jit(solution)/shard_map/psum | solution.py:64
  305.6 1.7 fusion.33
  307.4 1.4 convert_multiply_fusion
  308.8 24.0 %psum.22 = f32[3,32,32]{1,2,0:T(8,128)} all-reduce(f32[3,32,32]{1,2,0:T(8,128)} %fusion.33), channel_id=1, replica_groups=mesh['node'=8,'grp'=4] {'node'}, use_global_device_ids=true, to_apply=%region_1.0 | all-reduce | flops 3072 | bytes 24576 | tf_op jit(solution)/shard_map/psum | solution.py:66
  332.9 1.4 slice_bitcast_fusion.14
  334.2 0.8 copy.20
  335.0 1.4 copy.22
  336.4 1.4 copy.21
  337.8 1.4 fusion.39
  339.2 3.6 cholesky.59
  342.9 0.6 compare_reduce_fusion.2
  343.5 1.3 fusion.34
  344.8 3.8 custom-call.7
  348.5 3.6 cholesky.70
  352.2 0.6 compare_reduce_fusion.1
  352.9 1.3 fusion.35
  354.1 3.2 custom-call.8
  357.3 1.6 fusion.32
  358.9 1.6 fusion.31
  360.5 3.6 cholesky.81
  364.1 0.6 compare_reduce_fusion
  364.8 1.3 fusion.36
  366.0 3.2 custom-call.9
  369.2 1.0 fusion.30
  370.2 0.7 convolution_bitcast_fusion.2
  370.9 1.4 convolution_bitcast_fusion.3
  372.3 0.7 convolution_bitcast_fusion.4
  373.0 0.8 pad_maximum_fusion.2
  373.8 5.7 %fusion = bf16[384,1792]{1,0:T(8,128)(2,1)} fusion(f32[384,1792]{1,0:T(8,128)} %fusion.46, bf16[384,1024]{1,0:T(8,128)(2,1)S(1)} %get-tuple-element.8, bf16[1792,1024]{1,0:T(8,128)(2,1)} %all-gather.8.cloned.1.call-done), kind=kOutput, calls=%fused_computation.1 | convolution fusion | flops 1410662400 | bytes 8585216 | tf_op jit(solution)/shard_map/dot_general | solution.py:46
  379.5 0.6 pad_maximum_fusion.3
  380.2 119.2 %all-reduce.2.cloned.1.call-done = f32[3,1024,32]{1,2,0:T(8,128)} async-done(((f32[3,1024,32]{1,2,0:T(8,128)}), f32[3,1024,32]{1,2,0:T(8,128)}) %all-reduce.2.cloned.1.call-update) | async-done | bytes 393232 | tf_op jit(solution)/shard_map/psum | solution.py:72
  499.4 1.0 broadcast_multiply_fusion
  500.4 1.8 fusion.12
  502.2 0.9 fusion.13
  503.1 0.9 fusion.14
  504.1 1.2 pad_maximum_fusion.1
  (46 shorter events, 1.6 us)
Async XLA Ops:
  7.2 39.8 %all-gather.6.cloned.1.call-start = ((), (), s32[]{:S(2)}) async-start(), calls=%async_computation.2 | async-start | bytes 4128768 | tf_op jit(solution)/shard_map/all_gather | solution.py:33
  7.9 75.4 %all-gather.10.cloned.1.call-start = ((), (), s32[]{:S(2)}) async-start(), calls=%async_computation.4 | async-start | bytes 4128768 | tf_op jit(solution)/shard_map/all_gather | solution.py:31
  8.6 111.0 %all-gather.8.cloned.1.call-start = ((), (), s32[]{:S(2)}) async-start(), calls=%async_computation.3 | async-start | bytes 4128768 | tf_op jit(solution)/shard_map/all_gather | solution.py:32
  9.4 73.9 %copy-start.2 = (bf16[384,1792]{1,0:T(8,128)(2,1)S(1)}, bf16[384,1792]{1,0:T(8,128)(2,1)}, u32[]{:S(2)}) copy-start(bf16[384,1792]{1,0:T(8,128)(2,1)} %param.10) | copy-start | bytes 4128772
  9.4 194.9 %all-gather.14.cloned.1.call-start = ((), (), s32[]{:S(2)}) async-start(), calls=%async_computation.6 | async-start | bytes 7077888 | tf_op jit(solution)/shard_map/all_gather | solution.py:56
  126.0 0.9 copy-start.7
  126.0 148.4 %all-gather.12.cloned.1.call-start = ((), (), s32[]{:S(2)}) async-start(), calls=%async_computation.5 | async-start | bytes 14155776 | tf_op jit(solution)/shard_map/all_gather | solution.py:55
  128.2 1.3 copy-start.1
  131.1 29.4 %all-to-all-start.1 = ((bf16[384,8,224]{0,2,1:T(8,128)(2,1)}), bf16[384,8,224]{0,2,1:T(8,128)(2,1)S(1)}, u32[]{:S(2)}, u32[]{:S(2)}) async-start(bf16[384,8,224]{0,2,1:T(8,128)(2,1)} %bitcast.3), calls=%async_computation.1 | async-start | bytes 2752512 | tf_op jit(solution)/shard_map/all_to_all | solution.py:53
  160.5 37.1 %all-to-all-start = ((bf16[384,8,224]{0,2,1:T(8,128)(2,1)}), bf16[384,8,224]{0,2,1:T(8,128)(2,1)S(1)}, u32[]{:S(2)}, u32[]{:S(2)}) async-start(bf16[384,8,224]{0,2,1:T(8,128)(2,1)} %bitcast), calls=%async_computation | async-start | bytes 2752512 | tf_op jit(solution)/shard_map/all_to_all | solution.py:52
  164.1 335.3 %all-reduce.2.cloned.1.call-start = ((), (), s32[]{:S(2)}) async-start(), calls=%async_computation.7 | async-start | bytes 786432 | tf_op jit(solution)/shard_map/psum | solution.py:72
  197.6 1.3 copy-start.8
  198.9 5.4 %copy-start.4 = (bf16[8,28,8,384]{3,2,0,1:T(8,128)(2,1)S(1)}, bf16[8,28,8,384]{3,2,0,1:T(8,128)(2,1)}, u32[]{:S(2)}) copy-start(bf16[8,28,8,384]{3,2,0,1:T(8,128)(2,1)} %copy.25) | copy-start | bytes 4128772
  204.3 70.1 %copy-start.5 = (bf16[8,28,8,384]{3,2,0,1:T(8,128)(2,1)S(1)}, bf16[8,28,8,384]{3,2,0,1:T(8,128)(2,1)}, u32[]{:S(2)}) copy-start(bf16[8,28,8,384]{3,2,0,1:T(8,128)(2,1)} %copy.24) | copy-start | bytes 4128772
  274.4 6.4 %copy-start.3 = (bf16[1,224,3072]{2,1,0:T(8,128)(2,1)S(1)}, bf16[1,224,3072]{2,1,0:T(8,128)(2,1)}, u32[]{:S(2)}) copy-start(bf16[1,224,3072]{2,1,0:T(8,128)(2,1)} %param.15) | copy-start | bytes 4128772
  274.4 6.4 %copy-start.6 = (f32[224,1024]{1,0:T(8,128)S(1)}, f32[224,1024]{1,0:T(8,128)}, u32[]{:S(2)}) copy-start(f32[224,1024]{1,0:T(8,128)} %convolution_bitcast_fusion.1) | copy-start | bytes 2752516
  280.8 1.0 copy-start.16
  369.2 3.1 copy-start.9
  370.2 2.8 copy-start.14
  373.8 5.7 %copy-start.10 = (f32[32,224]{1,0:T(8,128)S(1)}, f32[32,224]{1,0:T(8,128)}, u32[]{:S(2)}) copy-start(f32[32,224]{1,0:T(8,128)} %fusion.32) | copy-start | bytes 86020
  373.8 5.7 %copy-start.12 = (f32[32,224]{1,0:T(8,128)S(1)}, f32[32,224]{1,0:T(8,128)}, u32[]{:S(2)}) copy-start(f32[32,224]{1,0:T(8,128)} %fusion.31) | copy-start | bytes 86020
  373.8 5.7 %copy-start.15 = (f32[32,224]{1,0:T(8,128)S(1)}, f32[32,224]{1,0:T(8,128)}, u32[]{:S(2)}) copy-start(f32[32,224]{1,0:T(8,128)} %copy-done.14) | copy-start | bytes 86020
  379.5 122.7 %copy-start.13 = (f32[32,224]{1,0:T(8,128)S(1)}, f32[32,224]{1,0:T(8,128)}, u32[]{:S(2)}) copy-start(f32[32,224]{1,0:T(8,128)} %fusion.31) | copy-start | bytes 86020
  500.4 3.7 copy-start
  500.4 2.7 copy-start.11
Sparse Core Ops, SparseCore 0:
  9.9 37.0 all-gather.5
  48.9 34.3 all-gather.9
  85.2 34.3 all-gather.7
  126.1 74.4 all-gather.13
  202.4 71.9 all-gather.11
  373.9 125.4 all-reduce.1
where the time goes:
time: 514 us; the launch traced here: 512 us
  waiting for transfers between devices  342 us (67%)
  matrix products  54.2 us (11%)
  blocking collectives  44.5 us (9%)
  other arithmetic  35.7 us (7%)
  between operations  14.4 us (3%)
  local copies, waits for them, and re-layouts  13.4 us (3%)
  starting transfers between devices  7.6 us (1%)
    psum x1, waiting for transfers between devices, on_device(): q_new = lax.psum(col_terms, ('node', 'grp')) / group_count  119 us
    all_gather x1, waiting for transfers between devices, on_device(): piece_gu = lax.all_gather(gate_up, 'node', axis=0, tiled=True)  64.7 us
    all_gather x1, waiting for transfers between devices, on_device(): lax.all_gather(down_weight_t, 'node', axis=0, tiled=True)  37.6 us
    all_to_all x1, waiting for transfers between devices, on_device(): lax.all_to_all(tokens, 'node', split_axis=1, concat_axis=0, tiled=True)  31.9 us
    all_gather x1, waiting for transfers between devices, on_device(): lax.all_gather(up_weight, 'node', axis=0, tiled=True)  31.5 us
    all_gather x1, waiting for transfers between devices, on_device(): lax.all_gather(gate_weight, 'node', axis=0, tiled=True)  31.1 us
    all_to_all x1, waiting for transfers between devices, on_device(): lax.all_to_all(cotangent, 'node', split_axis=1, concat_axis=0, tiled=True)  24.3 us
    psum x1, blocking collectives, on_device(): gram_matrix = lax.psum(local_gram, 'node')  24 us
  transfers between devices with their start and end apart: 8, of which 7 were waited for; matrix products, arithmetic and copies ran while one was open for 7% of the time, Pallas kernels for 0%

commit v1 on v0

--- a/solution.py
+++ b/solution.py
@@ -49,7 +49,12 @@
     ).astype(jnp.bfloat16)
     gate_up = jnp.concatenate([grad_gate, grad_up], axis=1)
     token_cols, cot_cols = (
-        lax.all_to_all(tokens, "node", split_axis=1, concat_axis=0, tiled=True),
+        jnp.concatenate(
+            lax.all_to_all(
+                jnp.stack(jnp.split(tokens, lax.axis_size("node"), axis=1)), "node", 0, 0
+            ),
+            axis=0,
+        ),
         lax.all_to_all(cotangent, "node", split_axis=1, concat_axis=0, tiled=True),
     )
     piece_gu = lax.all_gather(gate_up, "node", axis=0, tiled=True)

time: 514 us -> 498 us (0.969)
  waiting for transfers between devices: 342 us -> 329 us
  local copies, waits for them, and re-layouts: 13.4 us -> 22.3 us
  other arithmetic: 35.7 us -> 30.3 us
    all_to_all x1, waiting for transfers between devices: 24.3 us -> 11.1 us  [on_device(): lax.all_to_all(cotangent, 'node', split_axis=1, concat_axis=0, tiled=True)]
    unnamed x36 -> x58, local copies, waits for them, and re-layouts: 5.8 us -> 18.1 us
    all_gather x1, waiting for transfers between devices: 31.1 us -> 37.6 us  [on_device(): lax.all_gather(gate_weight, 'node', axis=0, tiled=True)]
    all_gather x1, waiting for transfers between devices: 37.6 us -> 31.1 us  [on_device(): lax.all_gather(down_weight_t, 'node', axis=0, tiled=True)]
  transfers between devices with their start and end apart: 8 -> 8, of which waited for: 7 -> 7; matrix products, arithmetic and copies ran while one was open for 7% -> 10% of each run, Pallas kernels for 0% -> 0%
where the time goes in v1:
time: 498 us; the launch traced here: 497 us
  waiting for transfers between devices  329 us (66%)
  matrix products  50.8 us (10%)
  blocking collectives  42.3 us (8%)
  other arithmetic  30.3 us (6%)
  local copies, waits for them, and re-layouts  22.3 us (4%)
  between operations  14.5 us (3%)
  starting transfers between devices  7.58 us (2%)
    psum x1, waiting for transfers between devices, on_device(): q_new = lax.psum(col_terms, ('node', 'grp')) / group_count  119 us
    all_gather x1, waiting for transfers between devices, on_device(): piece_gu = lax.all_gather(gate_up, 'node', axis=0, tiled=True)  64.7 us
    all_gather x1, waiting for transfers between devices, on_device(): lax.all_gather(gate_weight, 'node', axis=0, tiled=True)  37.6 us
    all_to_all x1, waiting for transfers between devices, on_device(): lax.all_to_all(jnp.stack(jnp.split(tokens, lax.axis_size('node'), axis=1)...  31.9 us
    all_gather x1, waiting for transfers between devices, on_device(): lax.all_gather(up_weight, 'node', axis=0, tiled=True)  31.5 us
    all_gather x1, waiting for transfers between devices, on_device(): lax.all_gather(down_weight_t, 'node', axis=0, tiled=True)  31.1 us
    psum x1, blocking collectives, on_device(): gram_matrix = lax.psum(local_gram, 'node')  22.9 us
    psum x1, blocking collectives, on_device(): lax.psum(row_terms.astype(jnp.bfloat16), 'grp').astype(jnp.float32)  19.4 us
  transfers between devices with their start and end apart: 8, of which 7 were waited for; matrix products, arithmetic and copies ran while one was open for 10% of the time, Pallas kernels for 0%

profile of v1, /device:TPU:0, one launch (start us, length us, event | category | flops | bytes accessed | tf_op | source)
XLA Modules:
  0.0 497.1 jit_solution(9300958166592846481)
XLA Ops:
  7.2 0.7 all-gather.10.cloned.1.call-update
  7.9 0.7 all-gather.6.cloned.1.call-update
  8.7 0.7 all-gather.8.cloned.1.call-update
  9.4 37.6 %all-gather.10.cloned.1.call-done = bf16[1792,1024]{1,0:T(8,128)(2,1)} async-done(((bf16[224,1024]{1,0:T(8,128)(2,1)}), bf16[1792,1024]{1,0:T(8,128)(2,1)}) %all-gather.10.cloned.1.call-update) | async-done | bytes 3670032 | tf_op jit(solution)/shard_map/all_gather | solution.py:31
  47.0 5.2 %fusion.46 = f32[384,1024]{1,0:T(8,128)} fusion(bf16[384,1792]{1,0:T(8,128)(2,1)} %param.10, bf16[1792,1024]{1,0:T(8,128)(2,1)} %all-gather.10.cloned.1.call-done), kind=kOutput, calls=%fused_computation.101 | convolution fusion | flops 1409286144 | bytes 6619136 | tf_op jit(solution)/shard_map/dot_general | solution.py:35
  52.2 31.1 %all-gather.6.cloned.1.call-done = bf16[1792,1024]{1,0:T(8,128)(2,1)} async-done(((bf16[224,1024]{1,0:T(8,128)(2,1)}), bf16[1792,1024]{1,0:T(8,128)(2,1)}) %all-gather.6.cloned.1.call-update) | async-done | bytes 3670032 | tf_op jit(solution)/shard_map/all_gather | solution.py:33
  83.3 4.8 fusion.45
  88.1 31.5 %all-gather.8.cloned.1.call-done = bf16[1792,1024]{1,0:T(8,128)(2,1)} async-done(((bf16[224,1024]{1,0:T(8,128)(2,1)}), bf16[1792,1024]{1,0:T(8,128)(2,1)}) %all-gather.8.cloned.1.call-update) | async-done | bytes 3670032 | tf_op jit(solution)/shard_map/all_gather | solution.py:32
  119.6 6.7 %multiply_convert_fusion = (bf16[384,1024]{1,0:T(8,128)(2,1)}, bf16[384,1024]{1,0:T(8,128)(2,1)}, bf16[384,1024]{1,0:T(8,128)(2,1)S(1)}) fusion(f32[384,1024]{1,0:T(8,128)} %fusion.46, f32[384,1024]{1,0:T(8,128)} %fusion.45, bf16[384,1792]{1,0:T(8,128)(2,1)S(1)} %copy-done, bf16[1792,1024]{1,0:T(8,128)(2,1)} %all-gather.8.cloned.1.call-done), kind=kOutput, calls=%fused_computation.14 | convolution fusion | flops 1419116544 | bytes 10551296 | tf_op jit(solution)/shard_map/dot_general | solution.py:36
  126.4 2.7 pad_maximum_fusion
  129.1 1.5 copy.44
  130.7 3.6 all-to-all-start.1
  134.3 1.3 fusion.44
  135.6 1.7 copy.51
  137.3 1.7 copy.52
  139.0 1.7 copy.53
  140.8 0.9 bitcast_dynamic-update-slice_fusion.7
  141.7 0.9 bitcast_dynamic-update-slice_fusion.6
  142.7 0.9 bitcast_dynamic-update-slice_fusion.5
  143.6 1.7 copy.54
  145.3 0.8 copy.55
  146.6 1.0 bitcast_dynamic-update-slice_fusion.4
  147.6 0.9 bitcast_dynamic-update-slice_fusion.3
  148.6 1.1 copy-done.1
  149.7 11.1 %all-to-all-done.1 = bf16[384,8,224]{0,2,1:T(8,128)(2,1)S(1)} async-done(((bf16[384,8,224]{0,2,1:T(8,128)(2,1)}), bf16[384,8,224]{0,2,1:T(8,128)(2,1)S(1)}, u32[]{:S(2)}, u32[]{:S(2)}) %all-to-all-start.1) | async-done | bytes 1376288 | tf_op jit(solution)/shard_map/all_to_all | solution.py:58
  160.8 3.6 all-to-all-start
  164.7 1.3 copy.60
  166.0 31.9 %all-to-all-done = bf16[8,384,224]{1,2,0:T(8,128)(2,1)S(1)} async-done(((bf16[8,384,224]{1,2,0:T(8,128)(2,1)}), bf16[8,384,224]{1,2,0:T(8,128)(2,1)S(1)}, u32[]{:S(2)}, u32[]{:S(2)}) %all-to-all-start) | async-done | bytes 1376288 | tf_op jit(solution)/shard_map/all_to_all | solution.py:53
  197.9 1.3 copy.59
  199.2 5.4 %fusion.47 = f32[384,1792]{1,0:T(8,128)} fusion(bf16[384,1024]{1,0:T(8,128)(2,1)S(1)} %copy-done.10, bf16[1792,1024]{1,0:T(8,128)(2,1)} %all-gather.10.cloned.1.call-done), kind=kOutput, calls=%fused_computation.102 | convolution fusion | flops 1409286144 | bytes 7208960 | tf_op jit(solution)/shard_map/dot_general | solution.py:43
  204.6 5.4 %convolution_bitcast_fusion = f32[224,1024]{1,0:T(8,128)} fusion(bf16[3072,224]{0,1:T(8,128)(2,1)S(1)} %bitcast.145, bf16[3072,1024]{1,0:T(8,128)(2,1)} %all-gather.14.cloned.1.call-done), kind=kOutput, calls=%fused_computation.18 | convolution fusion | flops 1409286144 | bytes 8585216 | tf_op jit(solution)/shard_map/dot_general | solution.py:20
  210.0 64.7 %all-gather.12.cloned.1.call-done = bf16[3072,2048]{1,0:T(8,128)(2,1)} async-done(((bf16[384,2048]{1,0:T(8,128)(2,1)}), bf16[3072,2048]{1,0:T(8,128)(2,1)}) %all-gather.12.cloned.1.call-update) | async-done | bytes 12582928 | tf_op jit(solution)/shard_map/all_gather | solution.py:60
  274.8 6.4 %fusion.48 = f32[224,2048]{1,0:T(8,128)S(1)} fusion(bf16[3072,224]{0,1:T(8,128)(2,1)S(1)} %bitcast.146, bf16[3072,2048]{1,0:T(8,128)(2,1)} %all-gather.12.cloned.1.call-done), kind=kOutput, calls=%fused_computation.103 | convolution fusion | flops 2818572288 | bytes 15794176 | tf_op jit(solution)/shard_map/dot_general | solution.py:20
  282.1 0.9 fusion.17
  283.0 0.9 fusion.16
  283.9 0.9 fusion.15
  284.9 19.4 %psum.21 = bf16[3,224,32]{1,2,0:T(8,128)(2,1)S(1)} all-reduce(bf16[3,224,32]{1,2,0:T(8,128)(2,1)S(1)} %pad_maximum_fusion.4), channel_id=1, replica_groups=mesh['node'=8,'grp'=4] {'grp'}, use_global_device_ids=true, to_apply=%region_0.0 | all-reduce | flops 21504 | bytes 86016 | tf_op jit(solution)/shard_map/psum | solution.py:69
  304.5 22.9 %psum.22 = f32[3,32,32]{1,2,0:T(8,128)S(1)} all-reduce(f32[3,32,32]{1,2,0:T(8,128)S(1)} %fusion.33), channel_id=1, replica_groups=mesh['node'=8,'grp'=4] {'node'}, use_global_device_ids=true, to_apply=%region_1.0 | all-reduce | flops 3072 | bytes 24576 | tf_op jit(solution)/shard_map/psum | solution.py:71
  327.7 0.6 fusion.39
  328.3 2.9 cholesky.81
  331.3 0.6 compare_reduce_fusion
  331.9 0.7 fusion.36
  332.6 2.4 custom-call.9
  335.9 1.3 convolution_bitcast_fusion.1
  337.2 2.9 cholesky.70
  340.1 0.6 compare_reduce_fusion.1
  340.8 0.7 fusion.35
  341.4 2.4 custom-call.8
  344.8 1.3 convolution_bitcast_fusion.2
  346.1 3.6 cholesky.59
  349.7 0.6 compare_reduce_fusion.2
  350.4 1.2 fusion.34
  351.5 3.2 custom-call.7
  354.7 1.0 fusion.32
  356.3 0.7 convolution_bitcast_fusion.3
  357.0 1.7 pad_maximum_fusion.2
  358.8 5.7 %fusion = bf16[384,1792]{1,0:T(8,128)(2,1)} fusion(f32[384,1792]{1,0:T(8,128)} %fusion.47, bf16[384,1024]{1,0:T(8,128)(2,1)S(1)} %copy-done.9, bf16[1792,1024]{1,0:T(8,128)(2,1)} %all-gather.8.cloned.1.call-done), kind=kOutput, calls=%fused_computation.1 | convolution fusion | flops 1410662400 | bytes 8585216 | tf_op jit(solution)/shard_map/dot_general | solution.py:46
  364.5 0.6 pad_maximum_fusion.3
  365.1 119.2 %all-reduce.2.cloned.1.call-done = f32[3,1024,32]{1,2,0:T(8,128)} async-done(((f32[3,1024,32]{1,2,0:T(8,128)}), f32[3,1024,32]{1,2,0:T(8,128)}) %all-reduce.2.cloned.1.call-update) | async-done | bytes 393232 | tf_op jit(solution)/shard_map/psum | solution.py:77
  484.3 1.0 broadcast_multiply_fusion
  485.4 1.8 fusion.12
  487.1 0.9 fusion.13
  488.1 0.9 fusion.14
  489.0 1.2 pad_maximum_fusion.1
  (70 shorter events, 4.9 us)
Async XLA Ops:
  7.2 39.8 %all-gather.10.cloned.1.call-start = ((), (), s32[]{:S(2)}) async-start(), calls=%async_computation.4 | async-start | bytes 4128768 | tf_op jit(solution)/shard_map/all_gather | solution.py:31
  7.9 75.4 %all-gather.6.cloned.1.call-start = ((), (), s32[]{:S(2)}) async-start(), calls=%async_computation.2 | async-start | bytes 4128768 | tf_op jit(solution)/shard_map/all_gather | solution.py:33
  8.6 111.0 %all-gather.8.cloned.1.call-start = ((), (), s32[]{:S(2)}) async-start(), calls=%async_computation.3 | async-start | bytes 4128768 | tf_op jit(solution)/shard_map/all_gather | solution.py:32
  9.4 73.9 %copy-start.3 = (bf16[384,1792]{1,0:T(8,128)(2,1)S(1)}, bf16[384,1792]{1,0:T(8,128)(2,1)}, u32[]{:S(2)}) copy-start(bf16[384,1792]{1,0:T(8,128)(2,1)} %param.11) | copy-start | bytes 4128772
  9.4 195.2 %all-gather.14.cloned.1.call-start = ((), (), s32[]{:S(2)}) async-start(), calls=%async_computation.6 | async-start | bytes 7077888 | tf_op jit(solution)/shard_map/all_gather | solution.py:61
  52.2 67.4 %copy-start = (bf16[384,1792]{1,0:T(8,128)(2,1)S(1)}, bf16[384,1792]{1,0:T(8,128)(2,1)}, u32[]{:S(2)}) copy-start(bf16[384,1792]{1,0:T(8,128)(2,1)} %param.10) | copy-start | bytes 4128772
  126.3 2.8 copy-start.8
  126.3 148.4 %all-gather.12.cloned.1.call-start = ((), (), s32[]{:S(2)}) async-start(), calls=%async_computation.5 | async-start | bytes 14155776 | tf_op jit(solution)/shard_map/all_gather | solution.py:60
  130.7 30.2 %all-to-all-start.1 = ((bf16[384,8,224]{0,2,1:T(8,128)(2,1)}), bf16[384,8,224]{0,2,1:T(8,128)(2,1)S(1)}, u32[]{:S(2)}, u32[]{:S(2)}) async-start(bf16[384,8,224]{0,2,1:T(8,128)(2,1)} %bitcast.8), calls=%async_computation.1 | async-start | bytes 2752512 | tf_op jit(solution)/shard_map/all_to_all | solution.py:58
  148.6 1.1 copy-start.1
  160.8 37.1 %all-to-all-start = ((bf16[8,384,224]{1,2,0:T(8,128)(2,1)}), bf16[8,384,224]{1,2,0:T(8,128)(2,1)S(1)}, u32[]{:S(2)}, u32[]{:S(2)}) async-start(bf16[8,384,224]{1,2,0:T(8,128)(2,1)} %copy-done.1), calls=%async_computation | async-start | bytes 2752512 | tf_op jit(solution)/shard_map/all_to_all | solution.py:53
  164.4 319.9 %all-reduce.2.cloned.1.call-start = ((), (), s32[]{:S(2)}) async-start(), calls=%async_computation.7 | async-start | bytes 786432 | tf_op jit(solution)/shard_map/psum | solution.py:77
  166.0 33.2 %copy-start.10 = (bf16[384,1024]{1,0:T(8,128)(2,1)S(1)}, bf16[384,1024]{1,0:T(8,128)(2,1)}, u32[]{:S(2)}) copy-start(bf16[384,1024]{1,0:T(8,128)(2,1)} %get-tuple-element.7) | copy-start | bytes 2359300
  199.2 5.4 %copy-start.5 = (bf16[8,28,8,384]{3,2,0,1:T(8,128)(2,1)S(1)}, bf16[8,28,8,384]{3,2,0,1:T(8,128)(2,1)}, u32[]{:S(2)}) copy-start(bf16[8,28,8,384]{3,2,0,1:T(8,128)(2,1)} %copy.60) | copy-start | bytes 4128772
  204.6 70.1 %copy-start.6 = (bf16[8,28,8,384]{3,2,0,1:T(8,128)(2,1)S(1)}, bf16[8,28,8,384]{3,2,0,1:T(8,128)(2,1)}, u32[]{:S(2)}) copy-start(bf16[8,28,8,384]{3,2,0,1:T(8,128)(2,1)} %copy.59) | copy-start | bytes 4128772
  274.8 6.4 %copy-start.4 = (bf16[1,224,3072]{2,1,0:T(8,128)(2,1)S(1)}, bf16[1,224,3072]{2,1,0:T(8,128)(2,1)}, u32[]{:S(2)}) copy-start(bf16[1,224,3072]{2,1,0:T(8,128)(2,1)} %param.15) | copy-start | bytes 4128772
  274.8 6.4 %copy-start.7 = (f32[224,1024]{1,0:T(8,128)S(1)}, f32[224,1024]{1,0:T(8,128)}, u32[]{:S(2)}) copy-start(f32[224,1024]{1,0:T(8,128)} %convolution_bitcast_fusion) | copy-start | bytes 2752516
  281.1 1.0 copy-start.20
  304.3 39.6 %copy-start.19 = (f32[3,224,32]{1,2,0:T(8,128)}, f32[3,224,32]{1,2,0:T(8,128)S(1)}, u32[]{:S(2)}) copy-start(f32[3,224,32]{1,2,0:T(8,128)S(1)} %convert_multiply_fusion) | copy-start | bytes 258052
  335.3 0.6 copy-start.11
  344.1 0.6 copy-start.13
  344.8 14.0 %copy-start.9 = (bf16[384,1024]{1,0:T(8,128)(2,1)S(1)}, bf16[384,1024]{1,0:T(8,128)(2,1)}, u32[]{:S(2)}) copy-start(bf16[384,1024]{1,0:T(8,128)(2,1)} %copy-done.8) | copy-start | bytes 2359300
  355.7 0.6 copy-start.16
  358.8 5.7 %copy-start.12 = (f32[32,224]{1,0:T(8,128)S(1)}, f32[32,224]{1,0:T(8,128)}, u32[]{:S(2)}) copy-start(f32[32,224]{1,0:T(8,128)} %copy-done.11) | copy-start | bytes 86020
  358.8 5.7 %copy-start.14 = (f32[32,224]{1,0:T(8,128)S(1)}, f32[32,224]{1,0:T(8,128)}, u32[]{:S(2)}) copy-start(f32[32,224]{1,0:T(8,128)} %copy-done.13) | copy-start | bytes 86020
  358.8 5.7 %copy-start.17 = (f32[32,224]{1,0:T(8,128)S(1)}, f32[32,224]{1,0:T(8,128)}, u32[]{:S(2)}) copy-start(f32[32,224]{1,0:T(8,128)} %copy-done.16) | copy-start | bytes 86020
  364.5 122.7 %copy-start.15 = (f32[32,224]{1,0:T(8,128)S(1)}, f32[32,224]{1,0:T(8,128)}, u32[]{:S(2)}) copy-start(f32[32,224]{1,0:T(8,128)} %copy-done.13) | copy-start | bytes 86020
  485.4 3.7 copy-start.2
  485.4 2.7 copy-start.18
Sparse Core Ops, SparseCore 0:
  9.9 37.0 all-gather.9
  48.9 34.3 all-gather.5
  85.2 34.3 all-gather.7
  126.5 74.4 all-gather.13
  202.7 71.9 all-gather.11
  358.9 125.3 all-reduce.1
